TPU v7x, 32 devices: a whole 2x2x4 slice. The times are simulated.
32 devices in a mesh: row: 4 (over z), col: 8 (over y, x, core).
Axes of the slice: x: 2, y: 2, z: 4, core: 2. Of those that a mesh axis runs over, the one named last changes fastest.
Arguments:
- front_matrix: bfloat16 [32768, 32768], P('row', 'col'), may hold values from -0.03125 to 0.03125
- right_random: bfloat16 [32768, 128], P(('col', 'row')), may hold values from -32 to 32
- left_random: bfloat16 [32768, 128], P(('row', 'col')), may hold values from -32 to 32
- row_basis: bfloat16 [32768, 384], P('row'), may hold values from -1 to 1, as said below
- column_basis: bfloat16 [32768, 384], P('col'), may hold values from -1 to 1, as said below
Outputs:
- row_samples: float32 [128, 32768], P('col', 'row')
- column_samples: float32 [128, 32768], P('row', 'col')
- row_spread: float32 [64], P('row')
- column_spread: float32 [64], P('col')
Inputs may be any that keep to these rules, and one draw needn't show every extreme that they name: Within each leaf node's 512 rows, the columns of row_basis are orthonormal up to their rounding to bfloat16. Within each leaf node's 512 rows, the columns of column_basis are orthonormal up to their rounding to bfloat16.
All inputs are finite; a program needn't handle non-finite values.
Results may differ from a plain program's by a relative error of at most 0.0003.
Values may be sent and summed in bfloat16 or wider, within the bound.
No kernel may reach another device: no remote copies, remote signals or barrier semaphores. Data moves between devices by JAX's collectives and lax.ppermute only.
A program may use at most 128 MiB of HBM per device.

v0:
```python
import jax
import jax.numpy as jnp
from jax import lax
from jax.sharding import PartitionSpec as P

SAMPLES = 128
EARLIER = 384
NODE = 512


def project_out(samples, basis):
    count = samples.shape[0]
    nodes = basis.shape[0] // NODE
    shaped = samples.reshape(count, nodes, NODE)
    stacked = basis.astype(jnp.float32).reshape(nodes, NODE, EARLIER)
    coeffs = jnp.einsum("knr,nre->kne", shaped, stacked, precision=lax.Precision.HIGHEST)
    correction = jnp.einsum("kne,nre->knr", coeffs, stacked, precision=lax.Precision.HIGHEST)
    cleaned = shaped - correction
    squares = jnp.sum(cleaned * cleaned, axis=(0, 2))
    return (cleaned.reshape(count, nodes * NODE), squares)


def shards(front_matrix, right_random, left_random, row_basis, column_basis):
    row_partial = jnp.einsum(
        "jc,ij->ci",
        lax.all_gather(right_random, "row", axis=0, tiled=True),
        front_matrix,
        preferred_element_type=jnp.float32,
    )
    column_partial = jnp.einsum(
        "ic,ij->cj",
        lax.all_gather(left_random, "col", axis=0, tiled=True),
        front_matrix,
        preferred_element_type=jnp.float32,
    )
    row_mine = lax.psum_scatter(row_partial, "col", scatter_dimension=0, tiled=True)
    column_mine = lax.psum_scatter(column_partial, "row", scatter_dimension=0, tiled=True)
    row_samples, row_partial_sq = project_out(row_mine, row_basis)
    column_samples, column_partial_sq = project_out(column_mine, column_basis)
    row_total_sq = lax.psum(row_partial_sq, "col")
    column_total_sq = lax.psum(column_partial_sq, "row")
    row_spread = jnp.sqrt(row_total_sq / (SAMPLES * NODE))
    column_spread = jnp.sqrt(column_total_sq / (SAMPLES * NODE))
    return (row_samples, column_samples, row_spread, column_spread)


def solution(mesh):
    in_specs = (
        P("row", "col"),
        P(("col", "row"), None),
        P(("row", "col"), None),
        P("row", None),
        P("col", None),
    )
    out_specs = (P("col", "row"), P("row", "col"), P("row"), P("col"))
    return jax.shard_map(shards, mesh=mesh, in_specs=in_specs, out_specs=out_specs, check_vma=False)
```

profile of v0, /device:TPU:0, one launch (start us, length us, event | category | flops | bytes accessed | tf_op | source)
XLA Modules:
  0.0 207.1 jit_solution(11374009316376437406)
XLA Ops:
  7.2 0.0 copy-start
  7.2 0.0 all-gather.3.cloned.1.call-start
  7.2 0.7 all-gather.3.cloned.1.call-update
  7.9 0.0 all-gather.5.cloned.1.call-start
  8.0 0.7 all-gather.5.cloned.1.call-update
  8.7 0.0 reduce-scatter.3.cloned.1.call-start
  8.7 31.6 %all-gather.3.cloned.1.call-done = bf16[4096,128]{1,0:T(8,128)(2,1)} async-done(((bf16[1024,128]{1,0:T(8,128)(2,1)}), bf16[4096,128]{1,0:T(8,128)(2,1)}) %all-gather.3.cloned.1.call-update) | async-done | bytes 1048592 | tf_op jit(solution)/shard_map/all_gather | solution.py:26
  40.3 29.5 %fusion.6 = f32[128,8192]{1,0:T(8,128)} fusion(bf16[4096,128]{1,0:T(8,128)(2,1)} %all-gather.3.cloned.1.call-done, bf16[8192,4096]{1,0:T(8,128)(2,1)} %param.5), kind=kOutput, calls=%fused_computation.14 | convolution fusion | flops 8589934592 | bytes 72351744 | tf_op jit(solution)/shard_map/jc,ij->ci/dot_general | solution.py:24
  69.8 0.0 reduce-scatter.3.cloned.1.call-update
  69.8 0.2 reduce-scatter.5.cloned.1.call-start
  70.1 0.0 all-gather.5.cloned.1.call-done
  70.1 27.7 %fusion.7 = f32[128,4096]{1,0:T(8,128)} fusion(bf16[8192,128]{1,0:T(8,128)(2,1)} %all-gather.5.cloned.1.call-done, bf16[8192,4096]{1,0:T(8,128)(2,1)} %param.5), kind=kOutput, calls=%fused_computation.15 | convolution fusion | flops 8589934592 | bytes 71303168 | tf_op jit(solution)/shard_map/ic,ij->cj/dot_general | solution.py:30
  97.7 0.0 reduce-scatter.5.cloned.1.call-update
  97.8 26.1 %reduce-scatter.3.cloned.1.call-done = f32[16,8192]{1,0:T(8,128)} async-done(((f32[128,8192]{1,0:T(8,128)}), f32[16,8192]{1,0:T(8,128)}) %reduce-scatter.3.cloned.1.call-update) | async-done | bytes 524304 | tf_op jit(solution)/shard_map/reduce_scatter | solution.py:36
  123.9 0.0 copy-start.2
  123.9 5.6 %convolution_bitcast_fusion.3 = f32[16,16,384]{2,0,1:T(8,128)S(1)} fusion(bf16[16,512,384]{2,1,0:T(8,128)(2,1)} %bitcast.40, f32[2,16,8,512]{3,2,1,0:T(8,128)} %bitcast.45), kind=kOutput, calls=%fused_computation.5 | convolution fusion | flops 603979776 | bytes 7208960 | tf_op jit(solution)/shard_map/knr,nre->kne/dot_general | solution.py:16
  129.5 0.0 copy-done.2
  129.5 7.2 %multiply_reduce_fusion.1 = (f32[16]{0:T(128)S(1)}, f32[16,16,512]{2,0,1:T(8,128)S(1)}) fusion(f32[16,16,384]{2,0,1:T(8,128)S(1)} %convolution_bitcast_fusion.3, bf16[16,512,384]{2,1,0:T(8,128)(2,1)} %bitcast.41, f32[2,16,8,512]{3,2,1,0:T(8,128)S(1)} %bitcast.46), kind=kOutput, calls=%fused_computation.9 | convolution fusion | flops 604372992 | bytes 7733312 | tf_op jit(solution)/shard_map/kne,nre->knr/dot_general | solution.py:17
  136.7 0.8 copy.17
  137.5 32.2 %reduce-scatter.5.cloned.1.call-done = f32[32,4096]{1,0:T(8,128)} async-done(((f32[128,4096]{1,0:T(8,128)}), f32[32,4096]{1,0:T(8,128)}) %reduce-scatter.5.cloned.1.call-update) | async-done | bytes 524304 | tf_op jit(solution)/shard_map/reduce_scatter | solution.py:37
  169.7 0.0 copy-done
  169.7 0.0 copy-start.1
  169.7 2.6 %convolution_bitcast_fusion.2 = f32[32,8,384]{2,0,1:T(8,128)S(1)} fusion(bf16[8,512,384]{2,1,0:T(8,128)(2,1)S(1)} %bitcast.38, f32[4,8,8,512]{3,2,1,0:T(8,128)} %bitcast.43), kind=kOutput, calls=%fused_computation.4 | convolution fusion | flops 603979776 | bytes 4063232 | tf_op jit(solution)/shard_map/knr,nre->kne/dot_general | solution.py:16
  172.3 0.0 copy-done.1
  172.4 3.0 %multiply_reduce_fusion = (f32[8]{0:T(128)S(1)}, f32[32,8,512]{2,0,1:T(8,128)S(1)}) fusion(f32[32,8,384]{2,0,1:T(8,128)S(1)} %convolution_bitcast_fusion.2, bf16[8,512,384]{2,1,0:T(8,128)(2,1)S(1)} %bitcast.39, f32[4,8,8,512]{3,2,1,0:T(8,128)S(1)} %bitcast.44), kind=kOutput, calls=%fused_computation.8 | convolution fusion | flops 604372992 | bytes 4587552 | tf_op jit(solution)/shard_map/kne,nre->knr/dot_general | solution.py:17
  175.4 0.8 copy.18
  176.2 13.2 %psum.14 = f32[16]{0:T(128)S(1)} all-reduce(f32[16]{0:T(128)S(1)} %get-tuple-element.4), channel_id=1, replica_groups=mesh['row'=4,'col'=8] {'col'}, use_global_device_ids=true, to_apply=%region_3.0 | all-reduce | flops 16 | bytes 128 | tf_op jit(solution)/shard_map/psum | solution.py:40
  189.4 0.5 multiply_sqrt_fusion.1
  189.9 10.2 %psum.15 = f32[8]{0:T(128)S(1)} all-reduce(f32[8]{0:T(128)S(1)} %get-tuple-element.6), channel_id=1, replica_groups=mesh['row'=4,'col'=8] {'row'}, use_global_device_ids=true, to_apply=%region_5.0 | all-reduce | flops 8 | bytes 64 | tf_op jit(solution)/shard_map/psum | solution.py:41
  200.1 0.5 multiply_sqrt_fusion
Async XLA Ops:
  7.2 162.6 %copy-start = (bf16[4096,384]{1,0:T(8,128)(2,1)S(1)}, bf16[4096,384]{1,0:T(8,128)(2,1)}, u32[]{:S(2)}) copy-start(bf16[4096,384]{1,0:T(8,128)(2,1)} %param.9) | copy-start | bytes 9437188
  7.2 33.1 %all-gather.3.cloned.1.call-start = ((), (), s32[]{:S(2)}) async-start(), calls=%async_computation.2 | async-start | bytes 1310720 | tf_op jit(solution)/shard_map/all_gather | solution.py:26
  7.9 62.2 %all-gather.5.cloned.1.call-start = ((), (), s32[]{:S(2)}) async-start(), calls=%async_computation.4 | async-start | bytes 2359296 | tf_op jit(solution)/shard_map/all_gather | solution.py:32
  8.7 115.2 %reduce-scatter.3.cloned.1.call-start = ((), (), s32[]{:S(2)}) async-start(), calls=%async_computation.3 | async-start | bytes 4718592 | tf_op jit(solution)/shard_map/reduce_scatter | solution.py:36
  69.8 99.9 %reduce-scatter.5.cloned.1.call-start = ((), (), s32[]{:S(2)}) async-start(), calls=%async_computation.5 | async-start | bytes 2621440 | tf_op jit(solution)/shard_map/reduce_scatter | solution.py:37
  123.9 5.6 %copy-start.2 = (f32[16,8192]{1,0:T(8,128)S(1)}, f32[16,8192]{1,0:T(8,128)}, u32[]{:S(2)}) copy-start(f32[16,8192]{1,0:T(8,128)} %reduce-scatter.3.cloned.1.call-done) | copy-start | bytes 1572868
  169.7 2.6 %copy-start.1 = (f32[32,4096]{1,0:T(8,128)S(1)}, f32[32,4096]{1,0:T(8,128)}, u32[]{:S(2)}) copy-start(f32[32,4096]{1,0:T(8,128)} %reduce-scatter.5.cloned.1.call-done) | copy-start | bytes 1572868
Sparse Core Ops, SparseCore 0:
  9.6 30.6 all-gather.2
  42.2 27.1 all-gather.4
  72.7 51.1 reduce-scatter.2
  126.1 43.6 reduce-scatter.4
where the time goes:
time: 207 us
  waiting for transfers between devices  91.3 us (44%)
  matrix products  75.6 us (37%)
  blocking collectives  23.4 us (11%)
  between operations  13.8 us (7%)
    reduce_scatter x1, waiting for transfers between devices, shards(): lax.psum_scatter(column_partial, 'row', scatter_dimension=0, tiled=True)  32.2 us
    all_gather x1, waiting for transfers between devices, shards(): lax.all_gather(right_random, 'row', axis=0, tiled=True)  31.6 us
    dot_general x1, matrix products, shards(): jnp.einsum('jc,ij->ci', lax.all_gather(right_random, 'row', axis=0, tiled...  29.5 us
    dot_general x1, matrix products, shards(): jnp.einsum('ic,ij->cj', lax.all_gather(left_random, 'col', axis=0, tiled=...  27.7 us
    reduce_scatter x1, waiting for transfers between devices, shards(): lax.psum_scatter(row_partial, 'col', scatter_dimension=0, tiled=True)  26.1 us
    psum x1, blocking collectives, shards(): row_total_sq = lax.psum(row_partial_sq, 'col')  13.2 us
    dot_general x2, matrix products, project_out(): jnp.einsum('kne,nre->knr', coeffs, stacked, precision=lax.Precision.HIGHEST)  10.2 us
    psum x1, blocking collectives, shards(): column_total_sq = lax.psum(column_partial_sq, 'row')  10.2 us
  transfers between devices with their start and end apart: 4, of which 3 were waited for; matrix products, arithmetic and copies ran while one was open for 34% of the time, Pallas kernels for 0%

commit v1 on v0

--- a/solution.py
+++ b/solution.py
@@ -37,7 +37,11 @@
     column_mine = lax.psum_scatter(column_partial, "row", scatter_dimension=0, tiled=True)
     row_samples, row_partial_sq = project_out(row_mine, row_basis)
     column_samples, column_partial_sq = project_out(column_mine, column_basis)
-    row_total_sq = lax.psum(row_partial_sq, "col")
+    row_total_sq = row_partial_sq
+    for hop in (1, 2, 4):
+        row_total_sq = row_total_sq + lax.ppermute(
+            row_total_sq, "col", [(dev, dev ^ hop) for dev in range(8)]
+        )
     column_total_sq = lax.psum(column_partial_sq, "row")
     row_spread = jnp.sqrt(row_total_sq / (SAMPLES * NODE))
     column_spread = jnp.sqrt(column_total_sq / (SAMPLES * NODE))

time: 207 us -> 201 us (0.971)
  blocking collectives: 23.4 us -> 10.1 us
  starting transfers between devices: 0.34 us -> 2.9 us
  matrix products: 75.6 us -> 77.8 us
  local copies, waits for them, and re-layouts: 1.69 us -> 3.76 us
    psum x1 -> x0, blocking collectives: 13.2 us -> none  [shards(): row_total_sq = lax.psum(row_partial_sq, 'col')]
    ppermute x0 -> x3, starting transfers between devices: none -> 2.56 us  [shards(): lax.ppermute(row_total_sq, 'col', [(dev, dev ^ hop) for dev in range(8)])]
    dot_general x2, matrix products: 10.2 us -> 12.4 us  [project_out(): jnp.einsum('kne,nre->knr', coeffs, stacked, precision=lax.Precision.HIGHEST)]
    reshape x2, local copies, waits for them, and re-layouts: 1.67 us -> 3.74 us  [project_out(): return (cleaned.reshape(count, nodes * NODE), squares)]
  transfers between devices with their start and end apart: 4 -> 7, of which waited for: 3 -> 5; matrix products, arithmetic and copies ran while one was open for 34% -> 41% of each run, Pallas kernels for 0% -> 0%
where the time goes in v1:
time: 201 us
  waiting for transfers between devices  91.5 us (46%)
  matrix products  77.8 us (39%)
  between operations  13.8 us (7%)
  blocking collectives  10.1 us (5%)
  local copies, waits for them, and re-layouts  3.76 us (2%)
  starting transfers between devices  2.9 us (1%)
    all_gather x1, waiting for transfers between devices, shards(): lax.all_gather(right_random, 'row', axis=0, tiled=True)  31.6 us
    reduce_scatter x1, waiting for transfers between devices, shards(): lax.psum_scatter(column_partial, 'row', scatter_dimension=0, tiled=True)  31.5 us
    dot_general x1, matrix products, shards(): jnp.einsum('jc,ij->ci', lax.all_gather(right_random, 'row', axis=0, tiled...  29.5 us
    dot_general x1, matrix products, shards(): jnp.einsum('ic,ij->cj', lax.all_gather(left_random, 'col', axis=0, tiled=...  27.6 us
    reduce_scatter x1, waiting for transfers between devices, shards(): lax.psum_scatter(row_partial, 'col', scatter_dimension=0, tiled=True)  26.1 us
    dot_general x2, matrix products, project_out(): jnp.einsum('kne,nre->knr', coeffs, stacked, precision=lax.Precision.HIGHEST)  12.4 us
    psum x1, blocking collectives, shards(): column_total_sq = lax.psum(column_partial_sq, 'row')  10.1 us
    dot_general x2, matrix products, project_out(): jnp.einsum('knr,nre->kne', shaped, stacked, precision=lax.Precision.HIGHEST)  8.19 us
  transfers between devices with their start and end apart: 7, of which 5 were waited for; matrix products, arithmetic and copies ran while one was open for 41% of the time, Pallas kernels for 0%

profile of v1, /device:TPU:0, one launch (start us, length us, event | category | flops | bytes accessed | tf_op | source)
XLA Modules:
  0.0 200.9 jit_solution(3277345994689600)
XLA Ops:
  7.2 0.0 copy-start
  7.2 0.0 all-gather.3.cloned.1.call-start
  7.2 0.7 all-gather.3.cloned.1.call-update
  7.9 0.0 all-gather.5.cloned.1.call-start
  8.0 0.7 all-gather.5.cloned.1.call-update
  8.7 0.0 reduce-scatter.3.cloned.1.call-start
  8.7 31.6 %all-gather.3.cloned.1.call-done = bf16[4096,128]{1,0:T(8,128)(2,1)} async-done(((bf16[1024,128]{1,0:T(8,128)(2,1)}), bf16[4096,128]{1,0:T(8,128)(2,1)}) %all-gather.3.cloned.1.call-update) | async-done | bytes 1048592 | tf_op jit(solution)/shard_map/all_gather | solution.py:26
  40.3 29.5 %fusion.6 = f32[128,8192]{1,0:T(8,128)} fusion(bf16[4096,128]{1,0:T(8,128)(2,1)} %all-gather.3.cloned.1.call-done, bf16[8192,4096]{1,0:T(8,128)(2,1)} %param.5), kind=kOutput, calls=%fused_computation.14 | convolution fusion | flops 8589934592 | bytes 72351744 | tf_op jit(solution)/shard_map/jc,ij->ci/dot_general | solution.py:24
  69.8 0.0 reduce-scatter.3.cloned.1.call-update
  69.9 0.2 reduce-scatter.5.cloned.1.call-start
  70.1 0.0 all-gather.5.cloned.1.call-done
  70.1 27.6 %fusion.7 = f32[128,4096]{1,0:T(8,128)} fusion(bf16[8192,128]{1,0:T(8,128)(2,1)} %all-gather.5.cloned.1.call-done, bf16[8192,4096]{1,0:T(8,128)(2,1)} %param.5), kind=kOutput, calls=%fused_computation.15 | convolution fusion | flops 8589934592 | bytes 71303168 | tf_op jit(solution)/shard_map/ic,ij->cj/dot_general | solution.py:30
  97.8 0.0 reduce-scatter.5.cloned.1.call-update
  97.8 26.1 %reduce-scatter.3.cloned.1.call-done = f32[16,8192]{1,0:T(8,128)} async-done(((f32[128,8192]{1,0:T(8,128)}), f32[16,8192]{1,0:T(8,128)}) %reduce-scatter.3.cloned.1.call-update) | async-done | bytes 524304 | tf_op jit(solution)/shard_map/reduce_scatter | solution.py:36
  123.9 0.0 copy-start.2
  123.9 5.6 %convolution_bitcast_fusion.3 = f32[16,16,384]{2,0,1:T(8,128)S(1)} fusion(bf16[16,512,384]{2,1,0:T(8,128)(2,1)} %bitcast.40, f32[2,16,8,512]{3,2,1,0:T(8,128)} %bitcast.45), kind=kOutput, calls=%fused_computation.5 | convolution fusion | flops 603979776 | bytes 7208960 | tf_op jit(solution)/shard_map/knr,nre->kne/dot_general | solution.py:16
  129.5 0.0 copy-done.2
  129.5 8.7 %multiply_reduce_fusion.1 = (f32[16]{0:T(128)S(1)}, f32[16,16,512]{2,0,1:T(8,128)}) fusion(f32[16,16,384]{2,0,1:T(8,128)S(1)} %convolution_bitcast_fusion.3, bf16[16,512,384]{2,1,0:T(8,128)(2,1)} %bitcast.41, f32[2,16,8,512]{3,2,1,0:T(8,128)S(1)} %bitcast.46), kind=kOutput, calls=%fused_computation.9 | convolution fusion | flops 604372992 | bytes 7733312 | tf_op jit(solution)/shard_map/kne,nre->knr/dot_general | solution.py:17
  138.2 0.0 collective-permute-start
  138.2 31.5 %reduce-scatter.5.cloned.1.call-done = f32[32,4096]{1,0:T(8,128)} async-done(((f32[128,4096]{1,0:T(8,128)}), f32[32,4096]{1,0:T(8,128)}) %reduce-scatter.5.cloned.1.call-update) | async-done | bytes 524304 | tf_op jit(solution)/shard_map/reduce_scatter | solution.py:37
  169.7 0.0 copy-start.1
  169.7 0.0 copy-done
  169.7 2.6 %convolution_bitcast_fusion.2 = f32[32,8,384]{2,0,1:T(8,128)S(1)} fusion(bf16[8,512,384]{2,1,0:T(8,128)(2,1)S(1)} %bitcast.38, f32[4,8,8,512]{3,2,1,0:T(8,128)} %bitcast.43), kind=kOutput, calls=%fused_computation.4 | convolution fusion | flops 603979776 | bytes 4063232 | tf_op jit(solution)/shard_map/knr,nre->kne/dot_general | solution.py:16
  172.3 0.0 copy-done.1
  172.4 3.7 %multiply_reduce_fusion = (f32[8]{0:T(128)S(1)}, f32[32,8,512]{2,0,1:T(8,128)}) fusion(f32[32,8,384]{2,0,1:T(8,128)S(1)} %convolution_bitcast_fusion.2, bf16[8,512,384]{2,1,0:T(8,128)(2,1)S(1)} %bitcast.39, f32[4,8,8,512]{3,2,1,0:T(8,128)S(1)} %bitcast.44), kind=kOutput, calls=%fused_computation.8 | convolution fusion | flops 604372992 | bytes 4587552 | tf_op jit(solution)/shard_map/kne,nre->knr/dot_general | solution.py:17
  176.1 10.1 %psum.7 = f32[8]{0:T(128)S(1)} all-reduce(f32[8]{0:T(128)S(1)} %get-tuple-element.6), channel_id=1, replica_groups=mesh['row'=4,'col'=8] {'row'}, use_global_device_ids=true, to_apply=%region_4.0 | all-reduce | flops 8 | bytes 64 | tf_op jit(solution)/shard_map/psum | solution.py:45
  186.2 0.5 multiply_sqrt_fusion
  186.7 0.0 collective-permute-done
  186.7 1.3 collective-permute-start.1
  188.0 1.9 copy.18
  189.8 0.4 collective-permute-done.1
  190.3 1.3 collective-permute-start.2
  191.6 1.9 copy.17
  193.4 0.4 collective-permute-done.2
  193.8 0.5 multiply_sqrt_fusion.1
  (2 shorter events, 0.0 us)
Async XLA Ops:
  7.2 162.6 %copy-start = (bf16[4096,384]{1,0:T(8,128)(2,1)S(1)}, bf16[4096,384]{1,0:T(8,128)(2,1)}, u32[]{:S(2)}) copy-start(bf16[4096,384]{1,0:T(8,128)(2,1)} %param.9) | copy-start | bytes 9437188
  7.2 33.1 %all-gather.3.cloned.1.call-start = ((), (), s32[]{:S(2)}) async-start(), calls=%async_computation.2 | async-start | bytes 1310720 | tf_op jit(solution)/shard_map/all_gather | solution.py:26
  7.9 62.2 %all-gather.5.cloned.1.call-start = ((), (), s32[]{:S(2)}) async-start(), calls=%async_computation.4 | async-start | bytes 2359296 | tf_op jit(solution)/shard_map/all_gather | solution.py:32
  8.7 115.2 %reduce-scatter.3.cloned.1.call-start = ((), (), s32[]{:S(2)}) async-start(), calls=%async_computation.3 | async-start | bytes 4718592 | tf_op jit(solution)/shard_map/reduce_scatter | solution.py:36
  69.9 99.9 %reduce-scatter.5.cloned.1.call-start = ((), (), s32[]{:S(2)}) async-start(), calls=%async_computation.5 | async-start | bytes 2621440 | tf_op jit(solution)/shard_map/reduce_scatter | solution.py:37
  123.9 5.6 %copy-start.2 = (f32[16,8192]{1,0:T(8,128)S(1)}, f32[16,8192]{1,0:T(8,128)}, u32[]{:S(2)}) copy-start(f32[16,8192]{1,0:T(8,128)} %reduce-scatter.3.cloned.1.call-done) | copy-start | bytes 1572868
  138.2 48.5 %collective-permute-start = (f32[16]{0:T(128)S(1)}, f32[16]{0:T(128)S(1)}, u32[]{:S(2)}, u32[]{:S(2)}) collective-permute-start(f32[16]{0:T(128)S(1)} %get-tuple-element.4), channel_id=1, source_target_pairs={{0,1},{1,0},{2,3},{3,2},{4,5},{5,4},{6,7},{7,6},{8,9},{9,8},{10,11... | collective-permute-start | bytes 200 | tf_op jit(solution)/shard_map/ppermute | solution.py:42
  169.7 2.6 %copy-start.1 = (f32[32,4096]{1,0:T(8,128)S(1)}, f32[32,4096]{1,0:T(8,128)}, u32[]{:S(2)}) copy-start(f32[32,4096]{1,0:T(8,128)} %reduce-scatter.5.cloned.1.call-done) | copy-start | bytes 1572868
  186.7 3.6 %collective-permute-start.1 = (f32[16]{0:T(128)S(1)}, f32[16]{0:T(128)S(1)}, u32[]{:S(2)}, u32[]{:S(2)}) collective-permute-start(f32[16]{0:T(128)S(1)} %add.15), channel_id=1, source_target_pairs={{0,2},{1,3},{2,0},{3,1},{4,6},{5,7},{6,4},{7,5},{8,10},{9,11},{10,... | collective-permute-start | bytes 200 | tf_op jit(solution)/shard_map/ppermute | solution.py:42
  190.3 3.6 %collective-permute-start.2 = (f32[16]{0:T(128)S(1)}, f32[16]{0:T(128)S(1)}, u32[]{:S(2)}, u32[]{:S(2)}) collective-permute-start(f32[16]{0:T(128)S(1)} %add.16), channel_id=1, source_target_pairs={{0,4},{1,5},{2,6},{3,7},{4,0},{5,1},{6,2},{7,3},{8,12},{9,13},{10,... | collective-permute-start | bytes 200 | tf_op jit(solution)/shard_map/ppermute | solution.py:42
Sparse Core Ops, SparseCore 0:
  9.6 30.6 all-gather.2
  42.2 27.1 all-gather.4
  72.7 51.1 reduce-scatter.2
  126.1 43.6 reduce-scatter.4
